TPU v7x, 32 devices: a whole 2x2x4 slice. The times are simulated.
32 devices in a mesh: orb: 8 (over z, y), clu: 4 (over x, core).
Axes of the slice: x: 2, y: 2, z: 4, core: 2. Of those that a mesh axis runs over, the one named last changes fastest.
Arguments:
- integrals: bfloat16 [1024, 1024, 512], P('orb', 'clu'), may hold values from -1.1953125 to 1.1953125
- metric: bfloat16 [1024, 1024], P(None, 'orb'), may hold values from -0.1875 to 0.1875
- occ_energy: float32 [1024], replicated, may hold values from -2 to -0.5
- virt_energy: float32 [512], replicated, may hold values from 0.5 to 4
- orbital_order: int32 [4, 256], replicated, may hold values from 0 to 255, each once within a row
- pair_first: int32 [4, 8, 4], P('clu', 'orb'), may hold values from 0 to 31
- pair_second: int32 [4, 8, 4], replicated, may hold values from 0 to 255
- pair_live: int32 [4, 8, 4], P('clu', 'orb'), may hold values 0 or 1
Outputs:
- gamma: bfloat16 [1024, 1024, 512], P('orb', 'clu')
Inputs may be any that keep to these rules, and one draw needn't show every extreme that they name: `orbital_order`: each row is a permutation of 0 to 255. `pair_second`: slot s names an orbital of cluster s.
All inputs are finite; a program needn't handle non-finite values. No bound on the sum of `pair_live` on one device may be relied on, other than what follows from the above.
Results may differ from a plain program's by a relative error of at most 0.0052.
Values may be sent and summed in bfloat16 or wider, within the bound.
A program may use at most 256 MiB of HBM per device.

v0:
```python
import jax
import jax.numpy as jnp
from jax import lax
from jax.sharding import PartitionSpec as P


def on_device(
    integrals, metric, occ_energy, virt_energy, orbital_order, pair_first, pair_second, pair_live
):
    orb_count = lax.axis_size("orb")
    clu_count = lax.axis_size("clu")
    here_orb = lax.axis_index("orb")
    here_clu = lax.axis_index("clu")
    xs_rows, occ_count, virt_width = integrals.shape
    full_aux = metric.shape[0]
    owned_count = occ_count // orb_count
    slot_count = pair_second.shape[2]
    per_cluster = slot_count // clu_count
    own_order = lax.dynamic_index_in_dim(orbital_order, here_clu, 0, keepdims=False)
    inverse = (
        jnp.zeros((occ_count,), jnp.int32).at[own_order].set(jnp.arange(occ_count, dtype=jnp.int32))
    )
    permuted = jnp.take(integrals, own_order, axis=1).reshape(
        xs_rows, orb_count, owned_count, virt_width
    )
    own_raw = lax.all_to_all(permuted, "orb", split_axis=1, concat_axis=0, tiled=True).reshape(
        full_aux, owned_count, virt_width
    )
    wanted = lax.dynamic_slice_in_dim(pair_second, here_clu * per_cluster, per_cluster, 2)
    picked_rows = jnp.take(integrals, wanted.reshape(-1), axis=1)
    picked_rows = picked_rows.reshape(xs_rows, clu_count, orb_count, per_cluster, virt_width)
    delivered = lax.all_to_all(
        lax.all_to_all(picked_rows, "orb", split_axis=2, concat_axis=0, tiled=True),
        "clu",
        split_axis=1,
        concat_axis=1,
        tiled=True,
    )
    raw_rows = jnp.concatenate(
        [own_raw, delivered.reshape(full_aux, clu_count * per_cluster, virt_width)], axis=1
    )
    orbit_count = raw_rows.shape[1]
    flattened = raw_rows.reshape(full_aux, orbit_count * virt_width)
    fitted = lax.dot_general(
        lax.all_gather(metric, "orb", axis=1, tiled=True),
        flattened,
        (((0,), (0,)), ((), ())),
        preferred_element_type=jnp.float32,
    ).astype(jnp.bfloat16)
    fitted = fitted.reshape(full_aux, orbit_count, virt_width)
    own_fit = fitted[:, :owned_count]
    second_fit = fitted[:, owned_count:]
    first_slot = pair_first[0, 0]
    live_mask = pair_live[0, 0].astype(jnp.float32)
    owned_orbs = (
        lax.dynamic_slice_in_dim(own_order, here_orb * owned_count, owned_count)
        + here_clu * occ_count
    )
    first_orb = jnp.take(owned_orbs, first_slot)
    own_second = lax.dynamic_index_in_dim(
        lax.dynamic_index_in_dim(pair_second, here_clu, 0, keepdims=False),
        here_orb,
        0,
        keepdims=False,
    )
    second_orb = own_second + jnp.arange(slot_count, dtype=jnp.int32) // per_cluster * occ_count
    first_fit = jnp.take(own_fit, first_slot, axis=1)
    intersection = jnp.einsum(
        "xpa,xpb->pab", first_fit, second_fit, preferred_element_type=jnp.float32
    )
    denominator = (
        virt_energy[None, :, None]
        + virt_energy[None, None, :]
        - occ_energy[first_orb][:, None, None]
        - occ_energy[second_orb][:, None, None]
    )
    amplitude = (live_mask[:, None, None] * intersection / denominator).astype(jnp.bfloat16)
    contribution = jnp.einsum(
        "pab,xpb->xpa", amplitude, second_fit, preferred_element_type=jnp.float32
    )
    onehot = (first_slot[:, None] == jnp.arange(owned_count, dtype=jnp.int32)[None, :]).astype(
        jnp.float32
    )
    gamma_local = jnp.einsum(
        "xpa,pd->xda", contribution, onehot, precision=lax.Precision.HIGHEST
    ).astype(jnp.bfloat16)
    returned = lax.all_to_all(gamma_local, "orb", split_axis=0, concat_axis=1, tiled=True)
    return jnp.take(returned, inverse, axis=1)


def solution(mesh):
    in_specs = (
        P("orb", "clu", None),
        P(None, "orb"),
        P(),
        P(),
        P(),
        P("clu", "orb", None),
        P(),
        P("clu", "orb", None),
    )
    out_specs = P("orb", "clu", None)
    return jax.shard_map(
        on_device, mesh=mesh, in_specs=in_specs, out_specs=out_specs, check_vma=False
    )
```

profile of v0, /device:TPU:12, one launch (start us, length us, event | category | flops | bytes accessed | tf_op | source)
XLA Modules:
  0.0 2005.8 jit_solution(14349656001542156532)
XLA Ops:
  7.0 1.4 fusion.21
  8.6 12.7 gather_fusion
  21.4 9.0 copy_select_fusion
  30.4 6.5 all-to-all-start.1
  37.6 1.4 scatter_custom_fusion
  39.6 62.1 %gather_fusion.5 = bf16[256,128,512]{2,0,1:T(8,128)(2,1)} fusion(bf16[128,256,512]{2,1,0:T(8,128)(2,1)} %param.10, s32[1024]{0:T(1024)S(1)} %pad_clamp_fusion.5), kind=kCustom, calls=%fused_computation.clone | custom fusion | bytes 67109888 | tf_op jit(solution)/shard_map/jit(_take)/gather | solution.py:23
  102.2 24.9 %all-to-all-done.1 = bf16[128,4,8,1,512]{4,0,1,3,2:T(8,128)(2,1)} async-done(((bf16[128,4,8,1,512]{4,0,1,3,2:T(8,128)(2,1)}), bf16[128,4,8,1,512]{4,0,1,3,2:T(8,128)(2,1)}, u32[]{:S(2)}, u32[]{:S(2)}) %all-to-all-start.1) | async-done | bytes 4194336 | tf_op jit(solution)/shard_map/all_to_all | solution.py:33
  127.1 4.6 copy.19
  131.7 4.9 all-to-all-start.2
  136.6 23.1 %broadcast_select_fusion = bf16[256,128,512]{2,0,1:T(8,128)(2,1)} fusion(bf16[256,128,512]{2,0,1:T(8,128)(2,1)} %gather_fusion.5, pred[256]{0:T(512)(128)(4,1)S(1)} %get-tuple-element.13), kind=kLoop, calls=%fused_computation.12 | loop fusion | flops 16777216 | bytes 67109120 | tf_op jit(solution)/shard_map/jit(_take)/select_n | solution.py:23
  159.6 23.0 %copy.16 = bf16[128,8,32,512]{3,2,0,1:T(8,128)(2,1)} copy(bf16[128,8,32,512]{3,2,1,0:T(8,128)(2,1)} %bitcast.85) | data formatting | bytes 67108864 | tf_op jit(solution)/shard_map/reshape | solution.py:23
  182.6 2.1 all-to-all-done.2
  184.8 10.3 all-to-all-start
  195.1 0.7 all-gather.2.cloned.1.call-update
  195.8 0.9 dynamic-slice_reduce_fusion
  196.7 0.8 add_bitcast_fusion
  199.6 7.4 copy.34
  207.0 732.4 %all-to-all-done = bf16[128,8,32,512]{3,2,0,1:T(8,128)(2,1)} async-done(((bf16[128,8,32,512]{3,2,0,1:T(8,128)(2,1)}), bf16[128,8,32,512]{3,2,0,1:T(8,128)(2,1)}, u32[]{:S(2)}, u32[]{:S(2)}) %all-to-all-start) | async-done | bytes 33554464 | tf_op jit(solution)/shard_map/all_to_all | solution.py:26
  939.5 27.2 %pad_maximum_fusion = bf16[1024,36,512]{2,1,0:T(8,128)(2,1)} fusion(bf16[1024,4,512]{2,1,0:T(4,128)(2,1)} %bitcast.90, bf16[1024,32,512]{2,1,0:T(8,128)(2,1)} %bitcast.9), kind=kLoop, calls=%fused_computation.8 | loop fusion | flops 75497472 | bytes 75497472 | tf_op jit(solution)/shard_map/concatenate | solution.py:39
  966.7 55.4 %copy.22 = bf16[1024,36,512]{0,2,1:T(8,128)(2,1)} copy(bf16[1024,36,512]{2,1,0:T(8,128)(2,1)} %pad_maximum_fusion) | data formatting | bytes 75497472 | tf_op jit(solution)/shard_map/concatenate | solution.py:39
  1022.1 47.9 %convolution_convert_fusion = bf16[18432,1024]{1,0:T(8,128)(2,1)} fusion(bf16[1024,18432]{0,1:T(8,128)(2,1)} %bitcast.87, bf16[1024,1024]{1,0:T(8,128)(2,1)} %all-gather.2.cloned.1.call-done), kind=kOutput, calls=%fused_computation.9 | convolution fusion | flops 38673580032 | bytes 77594624 | tf_op jit(solution)/shard_map/dot_general | solution.py:44
  1070.0 23.4 %slice.22 = bf16[1024,32,512]{0,2,1:T(8,128)(2,1)} slice(bf16[1024,36,512]{0,2,1:T(8,128)(2,1)} %bitcast.88), slice={[0:1024], [0:32], [0:512]} | slice | bytes 67108864 | tf_op jit(solution)/shard_map/slice | solution.py:51
  1093.5 4.9 gather_fusion.1
  1098.4 12.7 convolution_bitcast_fusion
  1111.1 35.5 %convert_bitcast_fusion = bf16[1024,32,512]{2,1,0:T(8,128)(2,1)} fusion(f32[1024,4,512]{2,0,1:T(8,128)} %convolution_bitcast_fusion, s32[4]{0:T(128)S(1)} %bitcast.96), kind=kOutput, calls=%fused_computation.11 | convolution fusion | flops 822083712 | bytes 41943056 | tf_op jit(solution)/shard_map/xpa,pd->xda/dot_general | solution.py:84
  1146.7 10.9 all-to-all-start.3
  1157.6 718.1 %all-to-all-done.3 = bf16[1024,32,512]{2,1,0:T(8,128)(2,1)} async-done(((bf16[1024,32,512]{2,1,0:T(8,128)(2,1)}), bf16[1024,32,512]{2,1,0:T(8,128)(2,1)}, u32[]{:S(2)}, u32[]{:S(2)}) %all-to-all-start.3) | async-done | bytes 33554464 | tf_op jit(solution)/shard_map/all_to_all | solution.py:87
  1875.7 22.9 %copy.25 = bf16[8,128,32,512]{3,2,0,1:T(8,128)(2,1)} copy(bf16[8,128,32,512]{3,2,1,0:T(8,128)(2,1)} %bitcast.33) | data formatting | bytes 67108864 | tf_op jit(solution)/shard_map/all_to_all | solution.py:87
  1898.6 31.1 %copy.26 = bf16[128,256,512]{2,0,1:T(8,128)(2,1)} copy(bf16[128,256,512]{2,1,0:T(8,128)(2,1)} %bitcast.86) | data formatting | bytes 67108864 | tf_op jit(solution)/shard_map/all_to_all | solution.py:87
  1929.7 23.0 %gather_fusion.6 = bf16[256,128,512]{2,1,0:T(8,128)(2,1)} fusion(bf16[128,256,512]{2,0,1:T(8,128)(2,1)} %copy.26, s32[1024]{0:T(1024)S(1)} %pad_clamp_fusion), kind=kCustom, calls=%fused_computation.1.clone | custom fusion | bytes 67109888 | tf_op jit(solution)/shard_map/jit(_take)/gather | solution.py:88
  1952.7 22.8 %select_bitcast_fusion = bf16[128,256,512]{2,0,1:T(8,128)(2,1)} fusion(bf16[256,128,512]{2,1,0:T(8,128)(2,1)} %gather_fusion.6, pred[256]{0:T(512)(128)(4,1)S(1)} %copy-done.4), kind=kLoop, calls=%fused_computation.10 | loop fusion | flops 16777216 | bytes 67109120 | tf_op jit(solution)/shard_map/jit(_take)/select_n | solution.py:88
  1975.5 23.0 %copy.27 = bf16[128,256,512]{2,1,0:T(8,128)(2,1)} copy(bf16[128,256,512]{2,0,1:T(8,128)(2,1)} %select_bitcast_fusion) | data formatting | bytes 67108864 | tf_op jit(solution)/shard_map/jit(_take)/select_n | solution.py:88
  (41 shorter events, 4.7 us)
Async XLA Ops:
  6.5 191.6 %copy-start = (f32[1024]{0:T(1024)S(1)}, f32[1024]{0:T(1024)}, u32[]{:S(2)}) copy-start(f32[1024]{0:T(1024)} %param.12) | copy-start | bytes 12292
  30.4 96.7 %all-to-all-start.1 = ((bf16[128,4,8,1,512]{4,0,1,3,2:T(8,128)(2,1)}), bf16[128,4,8,1,512]{4,0,1,3,2:T(8,128)(2,1)}, u32[]{:S(2)}, u32[]{:S(2)}) async-start(bf16[128,4,8,1,512]{4,0,1,3,2:T(8,128)(2,1)} %copy_select_fusion), calls=%async_computation.1 | async-start | bytes 8388608 | tf_op jit(solution)/shard_map/all_to_all | solution.py:33
  131.7 53.1 %all-to-all-start.2 = ((bf16[1024,4,1,1,512]{4,0,3,2,1:T(8,128)(2,1)}), bf16[1024,4,1,1,512]{4,0,3,2,1:T(8,128)(2,1)}, u32[]{:S(2)}, u32[]{:S(2)}) async-start(bf16[1024,4,1,1,512]{4,0,3,2,1:T(8,128)(2,1)} %bitcast.92), calls=%async_computation.2 | async-start | bytes 8388608 | tf_op jit(solution)/shard_map/all_to_all | solution.py:32
  182.6 14.9 copy-start.5
  182.6 16.9 copy-start.7
  182.6 16.9 copy-start.2
  184.8 754.7 %all-to-all-start = ((bf16[128,8,32,512]{3,2,0,1:T(8,128)(2,1)}), bf16[128,8,32,512]{3,2,0,1:T(8,128)(2,1)}, u32[]{:S(2)}, u32[]{:S(2)}) async-start(bf16[128,8,32,512]{3,2,0,1:T(8,128)(2,1)} %copy.16), calls=%async_computation | async-start | bytes 67108864 | tf_op jit(solution)/shard_map/all_to_all | solution.py:26
  195.1 827.0 %all-gather.2.cloned.1.call-start = ((), (), s32[]{:S(2)}) async-start(), calls=%async_computation.4 | async-start | bytes 2359296 | tf_op jit(solution)/shard_map/all_gather | solution.py:45
  1098.4 12.7 copy-start.6
  1146.6 10.9 copy-start.3
  1146.7 729.1 %all-to-all-start.3 = ((bf16[1024,32,512]{2,1,0:T(8,128)(2,1)}), bf16[1024,32,512]{2,1,0:T(8,128)(2,1)}, u32[]{:S(2)}, u32[]{:S(2)}) async-start(bf16[1024,32,512]{2,1,0:T(8,128)(2,1)} %convert_bitcast_fusion), calls=%async_computation.3 | async-start | bytes 67108864 | tf_op jit(solution)/shard_map/all_to_all | solution.py:87
  1929.7 23.0 %copy-start.4 = (pred[256]{0:T(512)(128)(4,1)S(1)}, pred[256]{0:T(512)(128)(4,1)}, u32[]{:S(2)}) copy-start(pred[256]{0:T(512)(128)(4,1)} %get-tuple-element.12) | copy-start | bytes 772
  1952.7 45.8 %copy-start.1 = (f32[1024]{0:T(1024)S(1)}, f32[1024]{0:T(1024)}, u32[]{:S(2)}) copy-start(f32[1024]{0:T(1024)} %param.12) | copy-start | bytes 12292
Sparse Core Ops, SparseCore 0:
  198.0 573.1 all-gather.1
where the time goes:
time: 2020 us; the launch traced here: 2010 us
  waiting for transfers between devices  1480 us (73%)
  local copies, waits for them, and re-layouts  300 us (15%)
  matrix products  96.2 us (5%)
  other arithmetic  84.9 us (4%)
  starting transfers between devices  32.6 us (2%)
    all_to_all x1, waiting for transfers between devices, on_device(): lax.all_to_all(permuted, 'orb', split_axis=1, concat_axis=0, tiled=True)  732 us
    all_to_all x1, waiting for transfers between devices, on_device(): lax.all_to_all(gamma_local, 'orb', split_axis=0, concat_axis=1, tiled=True)  718 us
    gather x1, local copies, waits for them, and re-layouts, on_device(): jnp.take(integrals, own_order, axis=1)  62.1 us
    concatenate x1, local copies, waits for them, and re-layouts, on_device(): jnp.concatenate([own_raw, delivered.reshape(full_aux, clu_count * per_clu...  55.4 us
    all_to_all x2, local copies, waits for them, and re-layouts, on_device(): lax.all_to_all(gamma_local, 'orb', split_axis=0, concat_axis=1, tiled=True)  54 us
    dot_general x1, matrix products, on_device(): lax.dot_general(lax.all_gather(metric, 'orb', axis=1, tiled=True), flatte...  47.9 us
  transfers between devices with their start and end apart: 5, of which 4 were waited for; matrix products, arithmetic and copies ran while one was open for 10% of the time, Pallas kernels for 0%

commit v1 on v0

v1 whole, which is shorter than its diff:
```python
import functools

import jax
import jax.numpy as jnp
from jax import lax
from jax.experimental import pallas as pl
from jax.experimental.pallas import tpu as pltpu
from jax.sharding import PartitionSpec as P

MESH = pl.DeviceIdType.MESH


def enter(orb, clu):
    barrier = pltpu.get_barrier_semaphore()
    d, c = lax.axis_index("orb"), lax.axis_index("clu")
    me = d * clu + c

    def greet(k, carry):
        to = lax.rem(me + k, orb * clu)
        pl.semaphore_signal(barrier, inc=1, device_id=(to // clu, lax.rem(to, clu)), device_id_type=MESH)
        return carry

    lax.fori_loop(1, orb * clu, greet, 0)
    pl.semaphore_wait(barrier, orb * clu - 1)


def gather_kernel(orb, clu, slots, per, xs, first_ref, second_ref, metric_ref, rows_ref, full_ref,
                  fs, fr, ss, sr, ms, mr, local):
    d, c = lax.axis_index("orb"), lax.axis_index("clu")
    me = d * clu + c
    enter(orb, clu)
    mine = pl.ds(pl.multiple_of(d * xs, xs), xs)

    def first_copy(to, at, sem):
        return pltpu.make_async_remote_copy(
            first_ref.at[to], rows_ref.at[pl.ds(0, slots), at], fs.at[to], fr.at[sem],
            device_id=(to, c), device_id_type=MESH)

    def metric_copy(to, sem):
        return pltpu.make_async_remote_copy(
            metric_ref, full_ref.at[sem], ms.at[to], mr.at[sem], device_id=(to, c), device_id_type=MESH)

    def second_copy(to, at, cluster, sem):
        return pltpu.make_async_remote_copy(
            second_ref.at[to], rows_ref.at[pl.ds(slots + cluster * per, per), at], ss.at[to], sr.at[sem],
            device_id=(to // clu, lax.rem(to, clu)), device_id_type=MESH)

    own = [
        pltpu.make_async_copy(first_ref.at[d], rows_ref.at[pl.ds(0, slots), mine], local.at[0]),
        pltpu.make_async_copy(second_ref.at[me], rows_ref.at[pl.ds(slots + c * per, per), mine], local.at[1]),
        pltpu.make_async_copy(metric_ref, full_ref.at[d], local.at[2]),
    ]
    for copy in own:
        copy.start()

    def start_orb(k, carry):
        to = lax.rem(d + k, orb)
        metric_copy(to, d).start()
        first_copy(to, mine, d).start()
        return carry

    def start_all(k, carry):
        to = lax.rem(me + k, orb * clu)
        second_copy(to, mine, c, me).start()
        return carry

    lax.fori_loop(1, orb, start_orb, 0)
    lax.fori_loop(1, orb * clu, start_all, 0)

    def end_orb(k, carry):
        to = lax.rem(d + k, orb)
        at = pl.ds(pl.multiple_of(to * xs, xs), xs)
        metric_copy(to, to).wait()
        first_copy(to, at, to).wait()
        return carry

    def end_all(k, carry):
        to = lax.rem(me + k, orb * clu)
        at = pl.ds(pl.multiple_of(to // clu * xs, xs), xs)
        second_copy(to, at, lax.rem(to, clu), to).wait()
        return carry

    lax.fori_loop(1, orb, end_orb, 0)
    lax.fori_loop(1, orb * clu, end_all, 0)
    for copy in own:
        copy.wait()


def return_kernel(orb, clu, xs, gamma_ref, back_ref, send, recv, local):
    d, c = lax.axis_index("orb"), lax.axis_index("clu")
    enter(orb, clu)

    def copy_to(to, sem):
        return pltpu.make_async_remote_copy(
            gamma_ref.at[:, pl.ds(pl.multiple_of(to * xs, xs), xs)], back_ref.at[sem], send.at[to], recv.at[sem],
            device_id=(to, c), device_id_type=MESH)

    own = pltpu.make_async_copy(
        gamma_ref.at[:, pl.ds(pl.multiple_of(d * xs, xs), xs)], back_ref.at[d], local.at[0])
    own.start()

    def start(k, carry):
        copy_to(lax.rem(d + k, orb), d).start()
        return carry

    def end(k, carry):
        to = lax.rem(d + k, orb)
        copy_to(to, to).wait()
        return carry

    lax.fori_loop(1, orb, start, 0)
    lax.fori_loop(1, orb, end, 0)
    own.wait()


def on_device(
    integrals, metric, occ_energy, virt_energy, orbital_order, pair_first, pair_second, pair_live
):
    orb, clu = lax.axis_size("orb"), lax.axis_size("clu")
    d, c = lax.axis_index("orb"), lax.axis_index("clu")
    xs, occ, virt = integrals.shape
    aux = metric.shape[0]
    owned = occ // orb
    slots = pair_second.shape[2]
    per = slots // clu
    any_space = pl.BlockSpec(memory_space=pl.ANY)
    dma = pltpu.SemaphoreType.DMA

    own_order = lax.dynamic_index_in_dim(orbital_order, c, 0, keepdims=False)
    all_first = lax.all_gather(pair_first[0, 0], "orb", axis=0, tiled=False)
    first_in = jnp.take_along_axis(own_order.reshape(orb, owned), all_first, axis=1)
    wanted = lax.dynamic_slice_in_dim(pair_second, c * per, per, 2).transpose(1, 0, 2)
    index = jnp.concatenate([first_in.reshape(-1), wanted.reshape(-1)])
    pick = (index[:, None] == jnp.arange(occ, dtype=jnp.int32)[None, :]).astype(jnp.bfloat16)
    picked = jnp.einsum("jo,poa->pja", pick, integrals).transpose(1, 0, 2)
    first_rows = picked[: orb * slots].reshape(orb, slots, xs, virt)
    second_rows = picked[orb * slots :].reshape(orb * clu, per, xs, virt)

    rows, full = pl.pallas_call(
        functools.partial(gather_kernel, orb, clu, slots, per, xs),
        out_shape=[
            jax.ShapeDtypeStruct((2 * slots, aux, virt), jnp.bfloat16),
            jax.ShapeDtypeStruct((orb,) + metric.shape, jnp.bfloat16),
        ],
        in_specs=[any_space] * 3,
        out_specs=[any_space] * 2,
        scratch_shapes=[dma((orb,)), dma((orb,)), dma((orb * clu,)), dma((orb * clu,)), dma((orb,)), dma((orb,)), dma((3,))],
        compiler_params=pltpu.CompilerParams(collective_id=0, has_side_effects=True),
    )(first_rows, second_rows, metric)

    whole_metric = full.transpose(0, 2, 1).reshape(aux, aux)
    fitted = jnp.einsum("qp,spa->sqa", whole_metric, rows, preferred_element_type=jnp.float32).astype(jnp.bfloat16)
    first_fit, second_fit = fitted[:slots], fitted[slots:]
    intersection = jnp.einsum("sqa,sqb->sab", first_fit, second_fit, preferred_element_type=jnp.float32)
    first_slot = pair_first[0, 0]
    live = pair_live[0, 0].astype(jnp.float32)
    first_orb = jnp.take(lax.dynamic_index_in_dim(first_in, d, 0, keepdims=False), jnp.arange(slots)) + c * occ
    own_second = lax.dynamic_index_in_dim(
        lax.dynamic_index_in_dim(pair_second, c, 0, keepdims=False), d, 0, keepdims=False)
    second_orb = own_second + jnp.arange(slots, dtype=jnp.int32) // per * occ
    denominator = (
        virt_energy[None, :, None]
        + virt_energy[None, None, :]
        - occ_energy[first_orb][:, None, None]
        - occ_energy[second_orb][:, None, None]
    )
    amplitude = (live[:, None, None] * intersection / denominator).astype(jnp.bfloat16)
    contribution = jnp.einsum("sab,sqb->sqa", amplitude, second_fit, preferred_element_type=jnp.float32)
    same = first_slot[:, None] == first_slot[None, :]
    gamma = []
    for s in range(slots):
        total = contribution[s]
        for t in range(slots):
            if t != s:
                total = total + jnp.where(same[s, t], contribution[t], 0.0)
        gamma.append(total.astype(jnp.bfloat16))
    gamma = jnp.stack(gamma)

    back = pl.pallas_call(
        functools.partial(return_kernel, orb, clu, xs),
        out_shape=jax.ShapeDtypeStruct((orb, slots, xs, virt), jnp.bfloat16),
        in_specs=[any_space],
        out_specs=any_space,
        scratch_shapes=[dma((orb,)), dma((orb,)), dma((1,))],
        compiler_params=pltpu.CompilerParams(collective_id=1, has_side_effects=True),
    )(gamma)

    earlier = (all_first[:, :, None] == all_first[:, None, :]) & (
        jnp.arange(slots)[None, :, None] > jnp.arange(slots)[None, None, :])
    speaks = ~jnp.any(earlier, axis=2)
    place = (
        (jnp.arange(occ, dtype=jnp.int32)[:, None] == first_in.reshape(-1)[None, :]) & speaks.reshape(-1)[None, :]
    ).astype(jnp.bfloat16)
    back = back.reshape(orb * slots, xs, virt).transpose(1, 0, 2)
    return jnp.einsum("oj,qja->qoa", place, back, preferred_element_type=jnp.float32).astype(jnp.bfloat16)


def solution(mesh):
    in_specs = (
        P("orb", "clu", None),
        P(None, "orb"),
        P(),
        P(),
        P(),
        P("clu", "orb", None),
        P(),
        P("clu", "orb", None),
    )
    out_specs = P("orb", "clu", None)
    return jax.shard_map(
        on_device, mesh=mesh, in_specs=in_specs, out_specs=out_specs, check_vma=False
    )
```

time: 2020 us -> 494 us (0.24)
  waiting for transfers between devices: 1480 us -> 0 us
  Pallas kernels: 0 us -> 348 us
  local copies, waits for them, and re-layouts: 300 us -> 65.6 us
  other arithmetic: 84.9 us -> 14.3 us
  matrix products: 96.2 us -> 50.4 us
  starting transfers between devices: 32.6 us -> 0 us
    all_to_all x4 -> x0, waiting for transfers between devices: 1480 us -> none  [the longest x1 732 us: on_device(): lax.all_to_all(permuted, 'orb', split_axis=1, concat_axis=0, tiled=True)]
    pallas_call x0 -> x2, Pallas kernels: none -> 348 us  [the longest x1 246 us: on_device(): pl.pallas_call(functools.partial(gather_kernel, orb, clu, slots, per, xs)...]
    gather x5 -> x6, local copies, waits for them, and re-layouts: 103 us -> 1.66 us  [the longest x5 1.01 us: on_device(): jnp.take_along_axis(own_order.reshape(orb, owned), all_first, axis=1)]
    all_to_all x4 -> x0, local copies, waits for them, and re-layouts: 66 us -> none  [the longest x2 54 us: on_device(): lax.all_to_all(gamma_local, 'orb', split_axis=0, concat_axis=1, tiled=True)]
    select_n x7 -> x1, other arithmetic: 56.1 us -> 0.01 us  [on_device(): jnp.take_along_axis(own_order.reshape(orb, owned), all_first, axis=1)]
    concatenate x1 -> x0, local copies, waits for them, and re-layouts: 55.4 us -> none  [on_device(): jnp.concatenate([own_raw, delivered.reshape(full_aux, clu_count * per_clu...]
    dot_general x3 -> x5, matrix products: 96.2 us -> 50.4 us  [the longest x1 17.2 us: on_device(): picked = jnp.einsum('jo,poa->pja', pick, integrals).transpose(1, 0, 2)]
    convert_element_type x0 -> x1, local copies, waits for them, and re-layouts: none -> 44 us  [on_device(): jnp.einsum('oj,qja->qoa', place, back, preferred_element_type=jnp.float32)]
  transfers between devices with their start and end apart: 5 -> 0, of which waited for: 4 -> 0; matrix products, arithmetic and copies ran while one was open for 10% -> 0% of each run, Pallas kernels for 0% -> 0%
where the time goes in v1:
time: 494 us; the launch traced here: 492 us
  Pallas kernels  348 us (70%)
  local copies, waits for them, and re-layouts  65.6 us (13%)
  matrix products  50.4 us (10%)
  blocking collectives  14.4 us (3%)
  other arithmetic  14.3 us (3%)
    pallas_call x1, Pallas kernels, on_device(): pl.pallas_call(functools.partial(gather_kernel, orb, clu, slots, per, xs)...  246 us
    pallas_call x1, Pallas kernels, on_device(): pl.pallas_call(functools.partial(return_kernel, orb, clu, xs), out_shape=...  101 us
    convert_element_type x1, local copies, waits for them, and re-layouts, on_device(): jnp.einsum('oj,qja->qoa', place, back, preferred_element_type=jnp.float32)  44 us
    dot_general x1, matrix products, on_device(): picked = jnp.einsum('jo,poa->pja', pick, integrals).transpose(1, 0, 2)  17.2 us
    dot_general x1, matrix products, on_device(): jnp.einsum('oj,qja->qoa', place, back, preferred_element_type=jnp.float32)  16.2 us
    all_gather x1, blocking collectives, on_device(): all_first = lax.all_gather(pair_first[0, 0], 'orb', axis=0, tiled=False)  14.4 us
    dot_general x1, matrix products, on_device(): jnp.einsum('qp,spa->sqa', whole_metric, rows, preferred_element_type=jnp....  11.6 us
    convert_element_type x2, other arithmetic, on_device(): gamma.append(total.astype(jnp.bfloat16))  10.1 us

profile of v1, /device:TPU:12, one launch (start us, length us, event | category | flops | bytes accessed | tf_op | source)
XLA Modules:
  0.0 492.4 jit_solution(3461599236508414716)
XLA Ops:
  0.0 0.7 copy-done
  0.7 0.2 dynamic-slice_reduce_fusion
  0.9 0.7 convert_bitcast_fusion.2
  1.5 0.8 broadcast_compare_fusion
  2.4 0.7 dynamic-slice_reduce_fusion.2
  3.3 14.4 %all-gather = s32[8,1,4]{2,1,0:T(1,128)S(1)} all-gather(s32[1,1,4]{2,1,0:T(1,128)} %param.13), channel_id=2, replica_groups=mesh['orb'=8,'clu'=4] {'orb'}, dimensions={0}, use_global_device_ids=true | all-gather | bytes 144 | tf_op jit(solution)/shard_map/all_gather | solution.py:130
  17.8 0.1 and_reduce_fusion
  17.9 0.1 copy.63
  18.0 0.1 not.11
  18.3 0.7 gather_fusion.3
  19.1 0.1 copy.53
  19.2 0.2 dynamic-slice_reduce_fusion.1
  19.3 0.6 gather_fusion
  20.3 0.6 gather_fusion.1
  20.9 0.6 gather_fusion.2
  21.5 0.7 fusion.19
  22.2 0.1 broadcast_add_fusion
  22.4 17.2 %fusion.7 = bf16[64,128,512]{2,0,1:T(8,128)(2,1)} fusion(bf16[128,256,512]{2,1,0:T(8,128)(2,1)} %param.8, s32[64]{0:T(128)S(1)} %pad_add_fusion), kind=kOutput, calls=%fused_computation.20 | convolution fusion | flops 2147500032 | bytes 41943296 | tf_op jit(solution)/shard_map/jo,poa->pja/dot_general | solution.py:135
  39.6 4.0 fusion.18
  43.6 4.3 copy.74
  47.9 4.4 copy.56
  52.3 246.3 %shard_map.82 = (bf16[8,1024,512]{2,1,0:T(8,128)(2,1)}, bf16[8,1024,128]{2,1,0:T(8,128)(2,1)}) custom-call(bf16[8,4,128,512]{3,2,1,0:T(8,128)(2,1)} %bitcast.68, bf16[32,1,128,512]{3,2,1,0:T(8,128)(2,1)} %bitcast.67, bf16[1024,128]{1,0:T(8,128)(2,1)} %metric_ref.1), custom_call_target="tpu_custom_call" | custom-call | tf_op jit(solution)/shard_map/pallas_call | solution.py:139
  298.6 2.9 copy.58
  301.5 11.6 %convert_bitcast_fusion.1 = bf16[8,1024,512]{1,2,0:T(8,128)(2,1)S(1)} fusion(bf16[8,1024,512]{2,1,0:T(8,128)(2,1)} %get-tuple-element.7, bf16[1024,1024,1]{1,0,2:T(8,128)(2,1)S(1)} %bitcast.70), kind=kOutput, calls=%fused_computation.5 | convolution fusion | flops 8594128896 | bytes 18874368 | tf_op jit(solution)/shard_map/qp,spa->sqa/dot_general | solution.py:152
  313.1 2.6 divide_convert_fusion
  315.7 2.8 fusion.20
  318.6 5.2 %add_convert_fusion.1 = (bf16[1,1024,512]{2,1,0:T(8,128)(2,1)S(1)}, bf16[1,1024,512]{2,1,0:T(8,128)(2,1)S(1)}) fusion(f32[4,1024,512]{2,1,0:T(8,128)S(1)} %fusion.20, pred[]{:T(512)} %bitcast.23, pred[]{:T(512)} %bitcast.22, pred[]{:T(512)} %bitcast.21, pred[]{:T(512)} %bitcast.26, pred[]{:T(512)} %bitcast.25, pred[]{:T(512)} %bitcast.24), kind=kLoop, calls=%fused_computation.14 | loop fusion | flops 7340032 | bytes 10485766 | tf_op jit(solution)/shard_map/convert_element_type | solution.py:176
  323.7 5.0 %add_convert_fusion.3 = (bf16[1,1024,512]{2,1,0:T(8,128)(2,1)S(1)}, bf16[1,1024,512]{2,1,0:T(8,128)(2,1)S(1)}) fusion(f32[4,1024,512]{2,1,0:T(8,128)S(1)} %fusion.20, pred[]{:T(512)} %bitcast.17, pred[]{:T(512)} %bitcast.16, pred[]{:T(512)} %bitcast.15, pred[]{:T(512)} %bitcast.20, pred[]{:T(512)} %bitcast.19, pred[]{:T(512)} %bitcast.18), kind=kLoop, calls=%fused_computation.16 | loop fusion | flops 7340032 | bytes 10485766 | tf_op jit(solution)/shard_map/convert_element_type | solution.py:176
  328.7 2.3 pad_maximum_fusion.gamma_ref
  331.0 101.3 %shard_map.83 = bf16[8,4,128,512]{3,2,1,0:T(8,128)(2,1)} custom-call(bf16[4,1024,512]{2,1,0:T(8,128)(2,1)} %pad_maximum_fusion.gamma_ref), custom_call_target="tpu_custom_call" | custom-call | tf_op jit(solution)/shard_map/pallas_call | solution.py:179
  432.3 16.2 %convert_bitcast_fusion = bf16[128,256,512]{1,2,0:T(8,128)(2,1)} fusion(bf16[32,128,512]{2,1,0:T(8,128)(2,1)} %bitcast.66, s32[32]{0:T(128)S(1)} %select_n.158, pred[32]{0:T(512)(128)(4,1)S(1)} %not.11), kind=kOutput, calls=%fused_computation.4 | convolution fusion | flops 1090535424 | bytes 37748896 | tf_op jit(solution)/shard_map/oj,qja->qoa/dot_general | solution.py:195
  448.5 44.0 %copy.64 = bf16[128,256,512]{2,1,0:T(8,128)(2,1)} copy(bf16[128,256,512]{1,2,0:T(8,128)(2,1)} %convert_bitcast_fusion) | data formatting | bytes 67108864 | tf_op jit(solution)/shard_map/convert_element_type | solution.py:195
  (27 shorter events, 0.9 us)
Async XLA Ops:
  0.0 0.7 copy-start
  0.0 20.3 %copy-start.2 = (f32[1024]{0:T(1024)S(1)}, f32[1024]{0:T(1024)}, u32[]{:S(2)}) copy-start(f32[1024]{0:T(1024)} %param.10) | copy-start | bytes 12292
  0.0 22.2 %copy-start.3 = (f32[512]{0:T(512)S(1)}, f32[512]{0:T(512)}, u32[]{:S(2)}) copy-start(f32[512]{0:T(512)} %param.11) | copy-start | bytes 6148
  448.5 44.0 %copy-start.1 = (s32[4,8,4]{1,2,0:T(4,128)S(1)}, s32[4,8,4]{1,2,0:T(4,128)}, u32[]{:S(2)}) copy-start(s32[4,8,4]{1,2,0:T(4,128)} %param.14) | copy-start | bytes 1540
